TPU v7x, 32 devices: a whole 2x2x4 slice. The times are simulated.
32 devices in a mesh: space: 16 (over z, y, core), tensor: 2 (over x).
Axes of the slice: x: 2, y: 2, z: 4, core: 2. Of those that a mesh axis runs over, the one named last changes fastest.
Arguments:
- tokens: bfloat16 [14336, 1024], P('space', 'tensor'), may hold values from -6 to 6
- first_weight: bfloat16 [1024, 1024], P(None, 'tensor'), may hold values from -0.1875 to 0.1875
- second_weight: bfloat16 [1024, 1024], P(None, 'tensor'), may hold values from -0.1875 to 0.1875
- head_weight: bfloat16 [352, 1024], P('tensor'), may hold values from -0.1875 to 0.1875
- targets: float32 [352, 14336], P('tensor', 'space'), may hold values from -6 to 6
- land_mask: int32 [4, 14336], P(None, 'space'), may hold values from 0 to 1, as said below
- variable_kind: int32 [88], P('tensor'), may hold values from 0 to 2
- loss_scale: float32 [], replicated, may hold values from 630784 to 5046272
Outputs:
- loss: float32 [], replicated
- token_grad: float32 [14336, 1024], P('space', 'tensor')
- first_grad: float32 [1024, 1024], P('space', 'tensor')
- second_grad: float32 [1024, 1024], P('space', 'tensor')
- head_grad: float32 [352, 1024], P('tensor', 'space')
Inputs may be any that keep to these rules, and one draw needn't show every extreme that they name: `land_mask`: every aligned group of 8 entries along the last dimension holds at least one 1 and one 0. `variable_kind`: 0 scores a variable on all cells, 1 on land cells, 2 on ocean cells.
All inputs are finite; a program needn't handle non-finite values.
Results may differ from a plain program's by a relative error of at most 0.0056.
Values may be sent and summed in bfloat16 or wider, within the bound.
A program may use at most 64 MiB of HBM per device.

v0:
```python
import math
import jax
import jax.numpy as jnp
from jax import lax
from jax.sharding import PartitionSpec as P

V = 88
PP = 4
PROW_DEV = 4
LONP = 224


def slope(z):
    cdf = 0.5 * (1.0 + lax.erf(z / math.sqrt(2.0)))
    return cdf + z * jnp.exp(-0.5 * z * z) / math.sqrt(2.0 * math.pi)


def column_folder(weights, piece):
    return lax.dot_general(
        piece, weights, (((1,), (1,)), ((), ())), preferred_element_type=jnp.float32
    )


def row_folder(weights, piece):
    return lax.dot_general(
        piece, weights, (((0,), (0,)), ((), ())), preferred_element_type=jnp.float32
    )


def per_device(
    tokens, first_weight, second_weight, head_weight, targets, land_mask, variable_kind, loss_scale
):
    count = tokens.shape[0]
    width = first_weight.shape[1]
    kinds = head_weight.shape[0] // PP
    rows_first, rows_second = (
        lax.all_to_all(first_weight, "tensor", split_axis=0, concat_axis=1, tiled=True),
        lax.all_to_all(second_weight, "tensor", split_axis=0, concat_axis=1, tiled=True),
    )
    head_cols = lax.all_to_all(head_weight, "tensor", split_axis=1, concat_axis=0, tiled=True)
    position = lax.axis_index("space") * count + jnp.arange(count, dtype=jnp.int32)
    cell = jnp.arange(PP, dtype=jnp.int32)
    lat_row = 2 * (position // LONP)[None, :] + (cell // 2)[:, None]
    nlat = 2 * PROW_DEV * lax.axis_size("space")
    cell_weight = jnp.cos(math.pi / 2.0 * (lat_row.astype(jnp.float32) + 0.5) / nlat)
    land = land_mask.astype(jnp.float32)
    kind = variable_kind[:, None, None]
    valid = jnp.where(kind == 0, 1.0, jnp.where(kind == 1, land[None], 1.0 - land[None]))
    masked = cell_weight[None] * valid
    local_weight = jnp.sum(masked, axis=(1, 2))
    weight_sum = lax.psum(local_weight, "space")
    full_in = lax.all_gather(tokens, "tensor", axis=1, tiled=True)
    pre_one = jnp.dot(full_in, first_weight, preferred_element_type=jnp.float32)
    hidden_one = jax.nn.gelu(pre_one, approximate=False).astype(jnp.bfloat16)
    full_one = lax.all_gather(hidden_one, "tensor", axis=1, tiled=True)
    pre_two = jnp.dot(full_one, second_weight, preferred_element_type=jnp.float32)
    hidden_two = jax.nn.gelu(pre_two, approximate=False).astype(jnp.bfloat16)
    full_two = lax.all_gather(hidden_two, "tensor", axis=1, tiled=True)
    predicted = lax.dot_general(
        head_weight, full_two, (((1,), (1,)), ((), ())), preferred_element_type=jnp.float32
    )
    error = predicted.reshape(kinds, PP, count) - targets.reshape(kinds, PP, count)
    local_error = jnp.sum(masked * error * error, axis=(1, 2))
    error_sum = lax.psum(local_error, "space")
    root = jnp.sqrt(error_sum / weight_sum + 1e-06)
    loss = lax.psum(jnp.sum(root), "tensor") / V
    coef = loss_scale / (V * root * weight_sum)
    grad_pred = (
        (coef[:, None, None] * masked * error).reshape(kinds * PP, count).astype(jnp.bfloat16)
    )
    back_two = row_folder(head_cols, lax.all_gather(grad_pred, "tensor", axis=0, tiled=True))
    head_term = jnp.dot(grad_pred, full_two, preferred_element_type=jnp.float32)
    head_grad = lax.psum_scatter(head_term, "space", scatter_dimension=1, tiled=True)
    grad_two = (back_two * slope(pre_two)).astype(jnp.bfloat16)
    back_one = column_folder(rows_second, lax.all_gather(grad_two, "tensor", axis=1, tiled=True))
    grad_one = (back_one * slope(pre_one)).astype(jnp.bfloat16)
    joined = lax.psum_scatter(
        jnp.concatenate(
            [
                lax.dot_general(
                    full_one, grad_two, (((0,), (0,)), ((), ())), preferred_element_type=jnp.float32
                ),
                lax.dot_general(
                    full_in, grad_one, (((0,), (0,)), ((), ())), preferred_element_type=jnp.float32
                ),
            ],
            axis=1,
        ),
        "space",
        scatter_dimension=0,
        tiled=True,
    )
    second_grad = joined[:, :width]
    first_grad = joined[:, width:]
    token_grad = column_folder(rows_first, lax.all_gather(grad_one, "tensor", axis=1, tiled=True))
    return (loss, token_grad, first_grad, second_grad, head_grad)


def solution(mesh):
    return jax.shard_map(
        per_device,
        mesh=mesh,
        in_specs=(
            P("space", "tensor"),
            P(None, "tensor"),
            P(None, "tensor"),
            P("tensor", None),
            P("tensor", "space"),
            P(None, "space"),
            P("tensor"),
            P(),
        ),
        out_specs=(
            P(),
            P("space", "tensor"),
            P("space", "tensor"),
            P("space", "tensor"),
            P("tensor", "space"),
        ),
        check_vma=False,
    )
```

profile of v0, /device:TPU:0, one launch (start us, length us, event | category | flops | bytes accessed | tf_op | source)
XLA Modules:
  0.0 390.4 jit_solution(11387166332372937541)
XLA Ops:
  7.2 0.7 all-gather.6.cloned.1.call-update
  8.0 34.5 %all-gather.6.cloned.1.call-done = bf16[896,1024]{1,0:T(8,128)(2,1)} async-done(((bf16[896,512]{1,0:T(8,128)(2,1)}), bf16[896,1024]{1,0:T(8,128)(2,1)}) %all-gather.6.cloned.1.call-update) | async-done | bytes 1835024 | tf_op jit(solution)/shard_map/all_gather | solution.py:52
  42.4 8.0 %fusion.2 = (bf16[896,512]{1,0:T(8,128)(2,1)}, f32[896,512]{1,0:T(8,128)}) fusion(bf16[896,1024]{1,0:T(8,128)(2,1)} %all-gather.6.cloned.1.call-done, bf16[1024,512]{1,0:T(8,128)(2,1)} %param.9), kind=kOutput, calls=%fused_computation.7 | convolution fusion | flops 969342976 | bytes 5636096 | tf_op jit(solution)/shard_map/dot_general | solution.py:53
  50.5 30.2 %all-gather.8.cloned.1.call-done = bf16[896,1024]{1,0:T(8,128)(2,1)} async-done(((bf16[896,512]{1,0:T(8,128)(2,1)}), bf16[896,1024]{1,0:T(8,128)(2,1)}) %all-gather.8.cloned.1.call-update) | async-done | bytes 1835024 | tf_op jit(solution)/shard_map/all_gather | solution.py:55
  80.7 7.5 %fusion.5 = (bf16[896,512]{1,0:T(8,128)(2,1)}, f32[896,512]{1,0:T(8,128)}) fusion(bf16[896,1024]{1,0:T(8,128)(2,1)} %all-gather.8.cloned.1.call-done, bf16[1024,512]{1,0:T(8,128)(2,1)S(1)} %copy-done.4), kind=kOutput, calls=%fused_computation.10 | convolution fusion | flops 969342976 | bytes 5636096 | tf_op jit(solution)/shard_map/dot_general | solution.py:56
  88.2 0.8 copy.33
  89.0 4.2 %all-to-all-start = ((bf16[176,2,512]{2,0,1:T(8,128)(2,1)}), bf16[176,2,512]{2,0,1:T(8,128)(2,1)}, u32[]{:S(2)}, u32[]{:S(2)}) async-start(bf16[176,2,512]{2,0,1:T(8,128)(2,1)} %bitcast.37), calls=%async_computation | async-start | bytes 720896 | tf_op jit(solution)/shard_map/all_to_all | solution.py:40
  93.3 0.2 multiply_cosine_fusion
  93.5 0.1 mul.116
  93.6 0.2 mul.117
  93.8 0.1 broadcast_in_dim.68
  93.9 0.2 broadcast_in_dim.69
  94.1 0.1 broadcast_in_dim.70
  94.2 0.2 broadcast_in_dim.71
  94.5 0.1 broadcast_in_dim.65
  94.5 0.1 broadcast_in_dim.66
  94.7 0.1 broadcast_in_dim.61
  94.7 0.1 broadcast_in_dim.62
  95.5 0.8 multiply_reduce_fusion
  96.3 23.1 %all-gather.10.cloned.1.call-done = bf16[896,1024]{1,0:T(8,128)(2,1)} async-done(((bf16[896,512]{1,0:T(8,128)(2,1)}), bf16[896,1024]{1,0:T(8,128)(2,1)}) %all-gather.10.cloned.1.call-update) | async-done | bytes 1835024 | tf_op jit(solution)/shard_map/all_gather | solution.py:58
  119.4 2.6 fusion.33
  122.0 0.1 reduce_sum.35
  122.1 0.1 reduce_sum.36
  122.2 33.2 %all-reduce = (f32[44]{0:T(128)S(1)}, f32[44]{0:T(128)S(1)}) all-reduce(f32[44]{0:T(128)S(1)} %reduce_sum.36, f32[44]{0:T(128)S(1)} %multiply_reduce_fusion), channel_id=1, replica_groups=mesh['space'=16,'tensor'=2] {'space'}, use_global_device_ids=true, to_apply=%region_2.3 | all-reduce | flops 88 | bytes 704 | tf_op jit(solution)/shard_map/psum | solution.py:64
  155.4 0.1 mul.131
  155.5 0.1 mul.132
  155.6 0.2 multiply_convert_fusion
  155.8 7.6 %all_gather.21 = bf16[352,896]{1,0:T(8,128)(2,1)S(1)} all-gather(bf16[176,896]{1,0:T(8,128)(2,1)S(1)} %multiply_convert_fusion), channel_id=1, replica_groups=mesh['space'=16,'tensor'=2] {'tensor'}, dimensions={0}, use_global_device_ids=true | all-gather | bytes 946176 | tf_op jit(solution)/shard_map/all_gather | solution.py:71
  163.4 3.7 fusion.11
  167.2 22.7 %all_to_all.57 = bf16[2,512,512]{2,1,0:T(8,128)(2,1)S(1)} all-to-all(bf16[2,512,512]{2,1,0:T(8,128)(2,1)S(1)} %bitcast.41), channel_id=1, replica_groups=mesh['space'=16,'tensor'=2] {'tensor'}, dimensions={0} | all-to-all | bytes 2097152 | tf_op jit(solution)/shard_map/all_to_all | solution.py:38
  189.9 0.5 copy.23
  190.4 8.6 %all-gather.12.cloned.1.call-done = bf16[896,1024]{1,0:T(8,128)(2,1)} async-done(((bf16[896,512]{1,0:T(8,128)(2,1)}), bf16[896,1024]{1,0:T(8,128)(2,1)}) %all-gather.12.cloned.1.call-update) | async-done | bytes 1835024 | tf_op jit(solution)/shard_map/all_gather | solution.py:75
  199.0 4.6 %fusion.17 = bf16[896,512]{1,0:T(8,128)(2,1)} fusion(f32[896,512]{1,0:T(8,128)} %get-tuple-element.36, bf16[896,1024]{1,0:T(8,128)(2,1)} %all-gather.12.cloned.1.call-done, bf16[512,1024]{0,1:T(8,128)(2,1)S(1)} %bitcast.44), kind=kOutput, calls=%fused_computation.22 | convolution fusion | flops 944111616 | bytes 5636096 | tf_op jit(solution)/shard_map/dot_general | solution.py:19
  203.7 3.2 fusion.38
  206.8 1.3 convolution_bitcast_fusion
  208.1 2.5 pad_maximum_fusion
  210.6 5.5 %copy.27 = f32[1024,1024]{1,0:T(8,128)} copy(f32[1024,1024]{0,1:T(8,128)} %pad_maximum_fusion) | data formatting | bytes 8388608
  216.2 3.7 all-to-all-start.2
  219.9 0.0 reduce-scatter.5.cloned.1.call-start
  220.0 1.9 fusion.39
  221.9 0.6 reduce_sum.38
  222.5 22.4 %all-to-all-done.2 = bf16[2,512,512]{2,1,0:T(8,128)(2,1)S(1)} async-done(((bf16[2,512,512]{2,1,0:T(8,128)(2,1)}), bf16[2,512,512]{2,1,0:T(8,128)(2,1)S(1)}, u32[]{:S(2)}, u32[]{:S(2)}) %all-to-all-start.2) | async-done | bytes 1048608 | tf_op jit(solution)/shard_map/all_to_all | solution.py:37
  244.9 0.5 copy.24
  245.4 5.6 %psum.23 = f32[]{:T(128)} all-reduce(f32[]{:T(128)} %reduce_sum.38), channel_id=1, replica_groups=mesh['space'=16,'tensor'=2] {'tensor'}, use_global_device_ids=true, to_apply=%region_6.7 | all-reduce | flops 1 | bytes 8 | tf_op jit(solution)/shard_map/psum | solution.py:66
  251.7 3.9 fusion.37
  255.5 66.0 %reduce-scatter.7.cloned.1.call-done = f32[64,1024]{1,0:T(8,128)} async-done(((f32[1024,1024]{1,0:T(8,128)}), f32[64,1024]{1,0:T(8,128)}) %reduce-scatter.7.cloned.1.call-update) | async-done | bytes 262160
  321.5 1.7 fusion.36
  323.2 59.2 %reduce-scatter.5.cloned.1.call-done = f32[176,64]{0,1:T(8,128)} async-done(((f32[176,1024]{0,1:T(8,128)}), f32[176,64]{0,1:T(8,128)}) %reduce-scatter.5.cloned.1.call-update) | async-done | bytes 45072 | tf_op jit(solution)/shard_map/reduce_scatter | solution.py:73
  (35 shorter events, 0.5 us)
Async XLA Ops:
  7.2 35.2 %all-gather.6.cloned.1.call-start = ((), (), s32[]{:S(2)}) async-start(), calls=%async_computation.5 | async-start | bytes 2752512 | tf_op jit(solution)/shard_map/all_gather | solution.py:52
  7.9 72.8 %copy-start.4 = (bf16[1024,512]{1,0:T(8,128)(2,1)S(1)}, bf16[1024,512]{1,0:T(8,128)(2,1)}, u32[]{:S(2)}) copy-start(bf16[1024,512]{1,0:T(8,128)(2,1)} %param.10) | copy-start | bytes 3145732
  7.9 72.8 %all-gather.8.cloned.1.call-start = ((), (), s32[]{:S(2)}) async-start(), calls=%async_computation.6 | async-start | bytes 2752512 | tf_op jit(solution)/shard_map/all_gather | solution.py:55
  50.4 37.8 %copy-start.3 = (bf16[176,1024]{1,0:T(8,128)(2,1)S(1)}, bf16[176,1024]{1,0:T(8,128)(2,1)}, u32[]{:S(2)}) copy-start(bf16[176,1024]{1,0:T(8,128)(2,1)} %param.11) | copy-start | bytes 1081348
  50.4 69.0 %all-gather.10.cloned.1.call-start = ((), (), s32[]{:S(2)}) async-start(), calls=%async_computation.7 | async-start | bytes 2752512 | tf_op jit(solution)/shard_map/all_gather | solution.py:58
  88.2 5.0 %copy-start.6 = (s32[4,896]{1,0:T(4,128)S(1)}, s32[4,896]{1,0:T(4,128)}, u32[]{:S(2)}) copy-start(s32[4,896]{1,0:T(4,128)} %param.13) | copy-start | bytes 43012
  89.0 74.4 %all-to-all-start = ((bf16[176,2,512]{2,0,1:T(8,128)(2,1)}), bf16[176,2,512]{2,0,1:T(8,128)(2,1)}, u32[]{:S(2)}, u32[]{:S(2)}) async-start(bf16[176,2,512]{2,0,1:T(8,128)(2,1)} %bitcast.37), calls=%async_computation | async-start | bytes 720896 | tf_op jit(solution)/shard_map/all_to_all | solution.py:40
  93.2 105.8 %all-gather.12.cloned.1.call-start = ((), (), s32[]{:S(2)}) async-start(), calls=%async_computation.8 | async-start | bytes 2752512 | tf_op jit(solution)/shard_map/all_gather | solution.py:75
  93.8 0.7 copy-start.7
  163.4 3.8 copy-start.5
  167.2 84.5 %all-gather.14.cloned.1.call-start = ((), (), s32[]{:S(2)}) async-start(), calls=%async_computation.9 | async-start | bytes 2752512 | tf_op jit(solution)/shard_map/all_gather | solution.py:95
  203.6 3.2 copy-start.1
  203.6 3.2 copy-start.2
  203.6 117.9 %reduce-scatter.7.cloned.1.call-start = ((), (), s32[]{:S(2)}) async-start(), calls=%async_computation.11 | async-start | bytes 4456448
  216.2 3.8 copy-start
  216.2 28.7 %all-to-all-start.2 = ((bf16[2,512,512]{2,1,0:T(8,128)(2,1)}), bf16[2,512,512]{2,1,0:T(8,128)(2,1)S(1)}, u32[]{:S(2)}, u32[]{:S(2)}) async-start(bf16[2,512,512]{2,1,0:T(8,128)(2,1)} %bitcast.42), calls=%async_computation.2 | async-start | bytes 2097152 | tf_op jit(solution)/shard_map/all_to_all | solution.py:37
  219.9 162.5 %reduce-scatter.5.cloned.1.call-start = ((), (), s32[]{:S(2)}) async-start(), calls=%async_computation.10 | async-start | bytes 1114112 | tf_op jit(solution)/shard_map/reduce_scatter | solution.py:73
Sparse Core Ops, SparseCore 0:
  9.5 32.8 all-gather.5
  50.5 30.1 all-gather.7
  88.3 31.0 all-gather.9
  167.3 31.6 all-gather.11
  203.7 40.9 all-gather.13
  248.5 72.9 reduce-scatter.6
  325.7 56.6 reduce-scatter.4
where the time goes:
time: 391 us; the launch traced here: 390 us
  waiting for transfers between devices  245 us (63%)
  blocking collectives  69.1 us (18%)
  matrix products  36.5 us (9%)
  between operations  16.8 us (4%)
  local copies, waits for them, and re-layouts  10.7 us (3%)
  starting transfers between devices  8.16 us (2%)
  other arithmetic  4.37 us (1%)
    unnamed x8, waiting for transfers between devices  66.7 us
    reduce_scatter x1, waiting for transfers between devices, per_device(): lax.psum_scatter(head_term, 'space', scatter_dimension=1, tiled=True)  59.2 us
    all_gather x1, waiting for transfers between devices, per_device(): full_in = lax.all_gather(tokens, 'tensor', axis=1, tiled=True)  34.5 us
    psum x1, blocking collectives, per_device(): error_sum = lax.psum(local_error, 'space')  33.2 us
    all_gather x1, waiting for transfers between devices, per_device(): full_one = lax.all_gather(hidden_one, 'tensor', axis=1, tiled=True)  30.2 us
    all_gather x1, waiting for transfers between devices, per_device(): full_two = lax.all_gather(hidden_two, 'tensor', axis=1, tiled=True)  23.1 us
    all_to_all x1, blocking collectives, per_device(): lax.all_to_all(second_weight, 'tensor', split_axis=0, concat_axis=1, tile...  22.7 us
    all_to_all x1, waiting for transfers between devices, per_device(): lax.all_to_all(first_weight, 'tensor', split_axis=0, concat_axis=1, tiled...  22.4 us
  transfers between devices with their start and end apart: 9, of which 7 were waited for; matrix products, arithmetic and copies ran while one was open for 7% of the time, Pallas kernels for 0%

commit v1 on v0

--- a/solution.py
+++ b/solution.py
@@ -8,6 +8,7 @@
 PP = 4
 PROW_DEV = 4
 LONP = 224
+_take_shifts_all = lambda values: jnp.concatenate(lax.all_gather(values, "tensor"), axis=1)
 
 
 def slope(z):
@@ -49,7 +50,7 @@
     masked = cell_weight[None] * valid
     local_weight = jnp.sum(masked, axis=(1, 2))
     weight_sum = lax.psum(local_weight, "space")
-    full_in = lax.all_gather(tokens, "tensor", axis=1, tiled=True)
+    full_in = _take_shifts_all(tokens)
     pre_one = jnp.dot(full_in, first_weight, preferred_element_type=jnp.float32)
     hidden_one = jax.nn.gelu(pre_one, approximate=False).astype(jnp.bfloat16)
     full_one = lax.all_gather(hidden_one, "tensor", axis=1, tiled=True)

time: 391 us -> 394 us (level)
  no operation moved by 1% of the time
where the time goes in v1:
time: 394 us
  waiting for transfers between devices  245 us (62%)
  blocking collectives  69.3 us (18%)
  matrix products  36.7 us (9%)
  between operations  16.8 us (4%)
  local copies, waits for them, and re-layouts  13.6 us (3%)
  starting transfers between devices  8.16 us (2%)
  other arithmetic  4.38 us (1%)
    unnamed x8, waiting for transfers between devices  66.7 us
    reduce_scatter x1, waiting for transfers between devices, per_device(): lax.psum_scatter(head_term, 'space', scatter_dimension=1, tiled=True)  59.2 us
    all_gather x1, waiting for transfers between devices, lax.all_gather(values, 'tensor')  34.5 us
    psum x1, blocking collectives, per_device(): error_sum = lax.psum(local_error, 'space')  33.2 us
    all_gather x1, waiting for transfers between devices, per_device(): full_one = lax.all_gather(hidden_one, 'tensor', axis=1, tiled=True)  30.2 us
    all_gather x1, waiting for transfers between devices, per_device(): full_two = lax.all_gather(hidden_two, 'tensor', axis=1, tiled=True)  23.1 us
    all_to_all x1, blocking collectives, per_device(): lax.all_to_all(second_weight, 'tensor', split_axis=0, concat_axis=1, tile...  22.7 us
    all_to_all x1, waiting for transfers between devices, per_device(): lax.all_to_all(first_weight, 'tensor', split_axis=0, concat_axis=1, tiled...  22.4 us
  transfers between devices with their start and end apart: 9, of which 7 were waited for; matrix products, arithmetic and copies ran while one was open for 7% of the time, Pallas kernels for 0%

profile of v1, /device:TPU:0, one launch (start us, length us, event | category | flops | bytes accessed | tf_op | source)
XLA Modules:
  0.0 393.6 jit_solution(17771153555626869735)
XLA Ops:
  7.2 0.7 all-gather.15.cloned.1.call-update
  7.9 34.5 %all-gather.15.cloned.1.call-done = bf16[1792,512]{1,0:T(8,128)(2,1)} async-done(((bf16[896,512]{1,0:T(8,128)(2,1)}), bf16[1792,512]{1,0:T(8,128)(2,1)}) %all-gather.15.cloned.1.call-update) | async-done | bytes 1835024 | tf_op jit(solution)/shard_map/all_gather | solution.py:11
  42.4 2.9 copy.23
  45.3 8.1 %fusion.2 = (bf16[896,512]{1,0:T(8,128)(2,1)}, f32[896,512]{1,0:T(8,128)}) fusion(bf16[896,1024]{0,1:T(8,128)(2,1)S(1)} %bitcast.44, bf16[1024,512]{1,0:T(8,128)(2,1)} %param.9), kind=kOutput, calls=%fused_computation.7 | convolution fusion | flops 969342976 | bytes 5636096 | tf_op jit(solution)/shard_map/dot_general | solution.py:54
  53.5 30.2 %all-gather.7.cloned.1.call-done = bf16[896,1024]{1,0:T(8,128)(2,1)} async-done(((bf16[896,512]{1,0:T(8,128)(2,1)}), bf16[896,1024]{1,0:T(8,128)(2,1)}) %all-gather.7.cloned.1.call-update) | async-done | bytes 1835024 | tf_op jit(solution)/shard_map/all_gather | solution.py:56
  83.7 7.5 %fusion.5 = (bf16[896,512]{1,0:T(8,128)(2,1)}, f32[896,512]{1,0:T(8,128)}) fusion(bf16[896,1024]{1,0:T(8,128)(2,1)} %all-gather.7.cloned.1.call-done, bf16[1024,512]{1,0:T(8,128)(2,1)S(1)} %copy-done.4), kind=kOutput, calls=%fused_computation.10 | convolution fusion | flops 969342976 | bytes 5636096 | tf_op jit(solution)/shard_map/dot_general | solution.py:57
  91.3 0.8 copy.35
  92.0 4.1 %all-to-all-start = ((bf16[176,2,512]{2,0,1:T(8,128)(2,1)}), bf16[176,2,512]{2,0,1:T(8,128)(2,1)}, u32[]{:S(2)}, u32[]{:S(2)}) async-start(bf16[176,2,512]{2,0,1:T(8,128)(2,1)} %bitcast.41), calls=%async_computation | async-start | bytes 720896 | tf_op jit(solution)/shard_map/all_to_all | solution.py:41
  96.3 0.2 multiply_cosine_fusion
  96.5 0.1 mul.116
  96.6 0.2 mul.117
  96.8 0.1 broadcast_in_dim.68
  96.9 0.2 broadcast_in_dim.69
  97.1 0.1 broadcast_in_dim.70
  97.2 0.2 broadcast_in_dim.71
  97.5 0.1 broadcast_in_dim.65
  97.5 0.1 broadcast_in_dim.66
  97.7 0.1 broadcast_in_dim.61
  97.7 0.1 broadcast_in_dim.62
  98.5 0.8 multiply_reduce_fusion
  99.3 23.1 %all-gather.9.cloned.1.call-done = bf16[896,1024]{1,0:T(8,128)(2,1)} async-done(((bf16[896,512]{1,0:T(8,128)(2,1)}), bf16[896,1024]{1,0:T(8,128)(2,1)}) %all-gather.9.cloned.1.call-update) | async-done | bytes 1835024 | tf_op jit(solution)/shard_map/all_gather | solution.py:59
  122.4 2.6 fusion.33
  125.0 0.1 reduce_sum.35
  125.1 0.1 reduce_sum.36
  125.2 33.2 %all-reduce = (f32[44]{0:T(128)S(1)}, f32[44]{0:T(128)S(1)}) all-reduce(f32[44]{0:T(128)S(1)} %reduce_sum.36, f32[44]{0:T(128)S(1)} %multiply_reduce_fusion), channel_id=1, replica_groups=mesh['space'=16,'tensor'=2] {'space'}, use_global_device_ids=true, to_apply=%region_2.3 | all-reduce | flops 88 | bytes 704 | tf_op jit(solution)/shard_map/psum | solution.py:65
  158.5 0.1 mul.131
  158.5 0.1 mul.132
  158.7 0.2 multiply_convert_fusion
  158.8 7.8 %all_gather.25 = bf16[352,896]{1,0:T(8,128)(2,1)S(1)} all-gather(bf16[176,896]{1,0:T(8,128)(2,1)S(1)} %multiply_convert_fusion), channel_id=1, replica_groups=mesh['space'=16,'tensor'=2] {'tensor'}, dimensions={0}, use_global_device_ids=true | all-gather | bytes 946176 | tf_op jit(solution)/shard_map/all_gather | solution.py:72
  166.6 3.7 fusion.11
  170.4 22.7 %all_to_all.57 = bf16[2,512,512]{2,1,0:T(8,128)(2,1)S(1)} all-to-all(bf16[2,512,512]{2,1,0:T(8,128)(2,1)S(1)} %bitcast.48), channel_id=1, replica_groups=mesh['space'=16,'tensor'=2] {'tensor'}, dimensions={0} | all-to-all | bytes 2097152 | tf_op jit(solution)/shard_map/all_to_all | solution.py:39
  193.2 0.5 copy.25
  193.7 8.5 %all-gather.11.cloned.1.call-done = bf16[896,1024]{1,0:T(8,128)(2,1)} async-done(((bf16[896,512]{1,0:T(8,128)(2,1)}), bf16[896,1024]{1,0:T(8,128)(2,1)}) %all-gather.11.cloned.1.call-update) | async-done | bytes 1835024 | tf_op jit(solution)/shard_map/all_gather | solution.py:76
  202.2 4.6 %fusion.17 = bf16[896,512]{1,0:T(8,128)(2,1)} fusion(f32[896,512]{1,0:T(8,128)} %get-tuple-element.36, bf16[896,1024]{1,0:T(8,128)(2,1)} %all-gather.11.cloned.1.call-done, bf16[512,1024]{0,1:T(8,128)(2,1)S(1)} %bitcast.51), kind=kOutput, calls=%fused_computation.22 | convolution fusion | flops 944111616 | bytes 5636096 | tf_op jit(solution)/shard_map/dot_general | solution.py:20
  206.9 3.2 fusion.38
  210.1 1.3 convolution_bitcast_fusion
  211.4 2.5 pad_maximum_fusion
  213.9 5.5 %copy.29 = f32[1024,1024]{1,0:T(8,128)} copy(f32[1024,1024]{0,1:T(8,128)} %pad_maximum_fusion) | data formatting | bytes 8388608
  219.5 3.7 all-to-all-start.2
  223.3 1.9 fusion.39
  225.1 0.6 reduce_sum.38
  225.7 22.4 %all-to-all-done.2 = bf16[2,512,512]{2,1,0:T(8,128)(2,1)S(1)} async-done(((bf16[2,512,512]{2,1,0:T(8,128)(2,1)}), bf16[2,512,512]{2,1,0:T(8,128)(2,1)S(1)}, u32[]{:S(2)}, u32[]{:S(2)}) %all-to-all-start.2) | async-done | bytes 1048608 | tf_op jit(solution)/shard_map/all_to_all | solution.py:38
  248.1 0.5 copy.26
  248.6 5.6 %psum.23 = f32[]{:T(128)} all-reduce(f32[]{:T(128)} %reduce_sum.38), channel_id=1, replica_groups=mesh['space'=16,'tensor'=2] {'tensor'}, use_global_device_ids=true, to_apply=%region_6.7 | all-reduce | flops 1 | bytes 8 | tf_op jit(solution)/shard_map/psum | solution.py:67
  254.9 3.9 fusion.37
  258.8 66.0 %reduce-scatter.7.cloned.1.call-done = f32[64,1024]{1,0:T(8,128)} async-done(((f32[1024,1024]{1,0:T(8,128)}), f32[64,1024]{1,0:T(8,128)}) %reduce-scatter.7.cloned.1.call-update) | async-done | bytes 262160
  324.7 1.7 fusion.36
  326.4 59.2 %reduce-scatter.5.cloned.1.call-done = f32[176,64]{0,1:T(8,128)} async-done(((f32[176,1024]{0,1:T(8,128)}), f32[176,64]{0,1:T(8,128)}) %reduce-scatter.5.cloned.1.call-update) | async-done | bytes 45072 | tf_op jit(solution)/shard_map/reduce_scatter | solution.py:74
  (38 shorter events, 0.5 us)
Async XLA Ops:
  7.2 35.2 %all-gather.15.cloned.1.call-start = ((), (), s32[]{:S(2)}) async-start(), calls=%async_computation.10 | async-start | bytes 2752512 | tf_op jit(solution)/shard_map/all_gather | solution.py:11
  7.9 75.8 %all-gather.7.cloned.1.call-start = ((), (), s32[]{:S(2)}) async-start(), calls=%async_computation.5 | async-start | bytes 2752512 | tf_op jit(solution)/shard_map/all_gather | solution.py:56
  45.3 8.1 %copy-start.1 = (bf16[896,2,512]{0,2,1:T(8,128)(2,1)}, bf16[896,2,512]{0,2,1:T(8,128)(2,1)S(1)}, u32[]{:S(2)}) copy-start(bf16[896,2,512]{0,2,1:T(8,128)(2,1)S(1)} %copy.23) | copy-start | bytes 5505028
  45.3 38.5 %copy-start.4 = (bf16[1024,512]{1,0:T(8,128)(2,1)S(1)}, bf16[1024,512]{1,0:T(8,128)(2,1)}, u32[]{:S(2)}) copy-start(bf16[1024,512]{1,0:T(8,128)(2,1)} %param.10) | copy-start | bytes 3145732
  53.4 37.8 %copy-start.3 = (bf16[176,1024]{1,0:T(8,128)(2,1)S(1)}, bf16[176,1024]{1,0:T(8,128)(2,1)}, u32[]{:S(2)}) copy-start(bf16[176,1024]{1,0:T(8,128)(2,1)} %param.11) | copy-start | bytes 1081348
  53.5 69.0 %all-gather.9.cloned.1.call-start = ((), (), s32[]{:S(2)}) async-start(), calls=%async_computation.6 | async-start | bytes 2752512 | tf_op jit(solution)/shard_map/all_gather | solution.py:59
  91.2 5.0 %copy-start.7 = (s32[4,896]{1,0:T(4,128)S(1)}, s32[4,896]{1,0:T(4,128)}, u32[]{:S(2)}) copy-start(s32[4,896]{1,0:T(4,128)} %param.13) | copy-start | bytes 43012
  92.0 74.6 %all-to-all-start = ((bf16[176,2,512]{2,0,1:T(8,128)(2,1)}), bf16[176,2,512]{2,0,1:T(8,128)(2,1)}, u32[]{:S(2)}, u32[]{:S(2)}) async-start(bf16[176,2,512]{2,0,1:T(8,128)(2,1)} %bitcast.41), calls=%async_computation | async-start | bytes 720896 | tf_op jit(solution)/shard_map/all_to_all | solution.py:41
  96.2 106.0 %all-gather.11.cloned.1.call-start = ((), (), s32[]{:S(2)}) async-start(), calls=%async_computation.7 | async-start | bytes 2752512 | tf_op jit(solution)/shard_map/all_gather | solution.py:76
  96.8 0.7 copy-start.8
  166.6 3.8 copy-start.5
  170.4 84.5 %all-gather.13.cloned.1.call-start = ((), (), s32[]{:S(2)}) async-start(), calls=%async_computation.8 | async-start | bytes 2752512 | tf_op jit(solution)/shard_map/all_gather | solution.py:96
  206.8 3.2 copy-start.2
  206.8 3.2 copy-start.6
  206.8 117.9 %reduce-scatter.7.cloned.1.call-start = ((), (), s32[]{:S(2)}) async-start(), calls=%async_computation.11 | async-start | bytes 4456448
  219.5 3.8 copy-start
  219.5 28.6 %all-to-all-start.2 = ((bf16[2,512,512]{2,1,0:T(8,128)(2,1)}), bf16[2,512,512]{2,1,0:T(8,128)(2,1)S(1)}, u32[]{:S(2)}, u32[]{:S(2)}) async-start(bf16[2,512,512]{2,1,0:T(8,128)(2,1)} %bitcast.49), calls=%async_computation.2 | async-start | bytes 2097152 | tf_op jit(solution)/shard_map/all_to_all | solution.py:38
  223.2 162.4 %reduce-scatter.5.cloned.1.call-start = ((), (), s32[]{:S(2)}) async-start(), calls=%async_computation.9 | async-start | bytes 1114112 | tf_op jit(solution)/shard_map/reduce_scatter | solution.py:74
Sparse Core Ops, SparseCore 0:
  9.5 32.8 all-gather.14
  53.6 30.1 all-gather.6
  91.4 31.0 all-gather.8
  170.5 31.6 all-gather.10
  206.9 40.9 all-gather.12
  251.7 73.0 reduce-scatter.6
  328.9 56.6 reduce-scatter.4
